TPU v7x, 32 devices: a whole 2x2x4 slice. The times are simulated.
32 devices in a mesh: seq: 16 (over z, y, core), batch: 2 (over x).
Axes of the slice: x: 2, y: 2, z: 4, core: 2. Of those that a mesh axis runs over, the one named last changes fastest.
Arguments:
- hidden_in: bfloat16 [2, 4096, 2304], P('batch', 'seq'), may hold values from -6 to 6
- segment_ids: int32 [2, 4096], P('batch', 'seq'), may hold values from 0 to 15, never falling along the last dimension, each value on 1 to 512 neighbouring positions
- pre_gain: float32 [2304], replicated, may hold values from 0.25 to 1.75
- w_qkv: bfloat16 [2304, 2048], P('seq'), may hold values from -0.27083333 to 0.27083333
- w_out: bfloat16 [1024, 2304], P('seq'), may hold values from -0.1875 to 0.1875
- post_gain: float32 [2304], replicated, may hold values from 0.25 to 1.75
Outputs:
- layer_out: bfloat16 [2, 4096, 2304], P('batch', 'seq')
Inputs may be any that keep to these rules, and one draw needn't show every extreme that they name: `segment_ids`: along each sequence the numbers never fall; a document is 1 to 512 positions long, and each sequence has one of exactly 512.
All inputs are finite; a program needn't handle non-finite values.
Results may differ from a plain program's by a relative error of at most 0.012.
The roundings to bfloat16 on the way count: a program that leaves them out, or rounds other values in their place, can miss the bound.
Values may be sent and summed in bfloat16 or wider, within the bound.
A program may use at most 128 MiB of HBM per device.

v0:
```python
import math
import jax
import jax.numpy as jnp
from jax import lax
from jax.sharding import PartitionSpec as P

Q_HEADS = 4
KV_HEADS = 2
HEAD = 256
WINDOW = 4096
DOCS = 16
EPS = 1e-06
CAP = 50.0


def from_behind(block, axis, distance):
    devices = range(lax.axis_size(axis))
    route = [(i - distance, i) for i in devices if i - distance in devices]
    return lax.ppermute(block, axis, route)


def rms_scale(values, gain):
    return values * lax.rsqrt(jnp.mean(values * values, axis=-1, keepdims=True) + EPS) * gain


def rotary(values, positions, leading):
    head_size = values.shape[-1]
    half_dim = head_size // 2
    inverse = 1.0 / 10000.0 ** (jnp.arange(half_dim, dtype=jnp.float32) * 2.0 / head_size)
    angles = positions.astype(jnp.float32)[:, None] * inverse[None, :]
    shape = (
        (1,) * leading + (positions.shape[0],) + (1,) * (values.ndim - 2 - leading) + (half_dim,)
    )
    cosine = jnp.cos(angles).reshape(shape)
    sine = jnp.sin(angles).reshape(shape)
    first_half = values[..., :half_dim]
    second_half = values[..., half_dim:]
    return jnp.concatenate(
        [first_half * cosine - second_half * sine, second_half * cosine + first_half * sine],
        axis=-1,
    )


def per_device(hidden_in, segment_ids, pre_gain, w_qkv, w_out, post_gain):
    tok_rows = hidden_in.shape[1]
    seq_count = lax.axis_size("seq")
    seq_index = lax.axis_index("seq")
    groups = Q_HEADS // KV_HEADS
    doc_most = min(WINDOW, seq_count * tok_rows // 8)
    hops = min(-(-(doc_most - 1) // tok_rows), seq_count - 1)
    positions = seq_index * tok_rows + jnp.arange(tok_rows, dtype=jnp.int32)
    own_ids = segment_ids[0]
    id_blocks = [from_behind(own_ids, "seq", d) for d in range(hops, 0, -1)] + [own_ids]
    widened = hidden_in[0].astype(jnp.float32)
    normed = rms_scale(widened, pre_gain).astype(jnp.bfloat16)
    projected = jnp.dot(
        normed, lax.all_gather(w_qkv, "seq", axis=0, tiled=True), preferred_element_type=jnp.float32
    )
    queries = rotary(
        projected[:, : Q_HEADS * HEAD].reshape(tok_rows, KV_HEADS, groups, HEAD), positions, 0
    ).astype(jnp.bfloat16)
    key_rows = rotary(
        projected[:, Q_HEADS * HEAD : (Q_HEADS + KV_HEADS) * HEAD].reshape(
            tok_rows, KV_HEADS, HEAD
        ),
        positions,
        0,
    ).astype(jnp.bfloat16)
    value_rows = projected[:, (Q_HEADS + KV_HEADS) * HEAD :].astype(jnp.bfloat16)
    both = jnp.concatenate([key_rows.reshape(tok_rows, KV_HEADS * HEAD), value_rows], axis=1)
    blocks = [from_behind(both, "seq", d) for d in range(hops, 0, -1)] + [both]
    kv = jnp.concatenate(blocks, axis=0).reshape(-1, 2, KV_HEADS, HEAD)
    ids = jnp.concatenate(id_blocks, axis=0)
    key_pos = (seq_index - hops) * tok_rows + jnp.arange((hops + 1) * tok_rows, dtype=jnp.int32)
    allowed = (
        (key_pos[None, :] >= 0)
        & (key_pos[None, :] <= positions[:, None])
        & (positions[:, None] - key_pos[None, :] < WINDOW)
        & (ids[None, :] == own_ids[:, None])
    )
    scores = jnp.einsum("qhgd,khd->hgqk", queries, kv[:, 0], preferred_element_type=jnp.float32) * (
        1.0 / math.sqrt(HEAD)
    )
    capped = CAP * jnp.tanh(scores / CAP)
    weights = jnp.where(allowed[None, None], jnp.exp(capped), 0.0)
    totals = jnp.sum(weights, axis=-1)
    mixed = jnp.einsum(
        "hgqk,khd->hgqd", weights.astype(jnp.bfloat16), kv[:, 1], preferred_element_type=jnp.float32
    )
    attended = (mixed / totals[..., None]).astype(jnp.bfloat16)
    attended = attended.transpose(2, 0, 1, 3).reshape(tok_rows, Q_HEADS * HEAD)
    branch = jnp.dot(
        attended,
        lax.all_gather(w_out, "seq", axis=0, tiled=True),
        preferred_element_type=jnp.float32,
    )
    return (widened + rms_scale(branch, post_gain)).astype(jnp.bfloat16)[None]


def solution(mesh):
    placed = (P("batch", "seq", None), P("batch", "seq"), P(), P("seq", None), P("seq", None), P())
    return jax.shard_map(
        per_device, mesh=mesh, in_specs=placed, out_specs=P("batch", "seq", None), check_vma=False
    )
```

profile of v0, /device:TPU:17, one launch (start us, length us, event | category | flops | bytes accessed | tf_op | source)
XLA Modules:
  0.0 167.0 jit_solution(11932889768963249122)
XLA Ops:
  6.5 0.0 all-gather.3.cloned.1.call-start
  6.5 0.7 all-gather.3.cloned.1.call-update
  7.3 0.0 all-gather.5.cloned.1.call-start
  7.3 0.7 all-gather.5.cloned.1.call-update
  8.0 3.7 %collective-permute-start.1 = (s32[256]{0:T(256)}, s32[256]{0:T(256)S(1)}, u32[]{:S(2)}, u32[]{:S(2)}) collective-permute-start(s32[256]{0:T(256)} %bitcast.51), channel_id=1, source_target_pairs={{0,2},{2,4},{4,6},{6,8},{8,10},{10,12},{12,14},{14,16},{16,18},{18... | collective-permute-start | bytes 3080 | tf_op jit(solution)/shard_map/ppermute | solution.py:19
  11.7 3.1 %collective-permute-start = (s32[256]{0:T(256)}, s32[256]{0:T(256)S(1)}, u32[]{:S(2)}, u32[]{:S(2)}) collective-permute-start(s32[256]{0:T(256)} %bitcast.52), channel_id=1, source_target_pairs={{0,4},{2,6},{4,8},{6,10},{8,12},{10,14},{12,16},{14,18},{16,20},{1... | collective-permute-start | bytes 3080 | tf_op jit(solution)/shard_map/ppermute | solution.py:19
  14.9 1.6 fusion
  16.5 1.3 multiply_cosine_fusion
  17.8 0.0 collective-permute-done.1
  17.8 0.0 collective-permute-done
  17.8 0.0 copy-done.9
  17.8 1.4 fusion.26
  19.2 72.1 %all-gather.3.cloned.1.call-done = bf16[2304,2048]{1,0:T(8,128)(2,1)} async-done(((bf16[144,2048]{1,0:T(8,128)(2,1)}), bf16[2304,2048]{1,0:T(8,128)(2,1)}) %all-gather.3.cloned.1.call-update) | async-done | bytes 9437200 | tf_op jit(solution)/shard_map/all_gather | solution.py:57
  91.3 0.0 copy-done
  91.3 0.0 copy-done.10
  91.3 5.2 %fusion.16 = f32[256,2048]{1,0:T(8,128)S(1)} fusion(bf16[2304,2048]{1,0:T(8,128)(2,1)} %all-gather.3.cloned.1.call-done, bf16[1,256,2304]{2,1,0:T(8,128)(2,1)S(1)} %copy-done, f32[2304]{0:T(1024)S(1)} %copy-done.10, f32[256]{0:T(256)S(1)} %add_rsqrt_fusion.1), kind=kOutput, calls=%fused_computation.19 | convolution fusion | flops 2418278400 | bytes 12724224 | tf_op jit(solution)/shard_map/dot_general | solution.py:56
  96.6 0.0 copy-start.2
  96.6 0.0 copy-start.3
  96.7 1.4 reshape.256
  98.0 0.0 copy-done.2
  98.0 0.0 copy-done.3
  98.0 1.4 subtract_convert_fusion.1
  99.5 0.3 pad_maximum_fusion.1
  99.8 0.9 pad_maximum_fusion
  100.7 2.4 %collective-permute-start.3 = (bf16[256,1024]{1,0:T(8,128)(2,1)}, bf16[256,1024]{1,0:T(8,128)(2,1)}, u32[]{:S(2)}, u32[]{:S(2)}) collective-permute-start(bf16[256,1024]{1,0:T(8,128)(2,1)} %pad_maximum_fusion), channel_id=1, source_target_pairs={{0,2},{2,4},{4,6},{6,8},{8,10},{10,12},{12,14},{14,16},{16,18},{18... | collective-permute-start | bytes 1572872 | tf_op jit(solution)/shard_map/ppermute | solution.py:19
  103.1 3.2 %collective-permute-start.2 = (bf16[256,1024]{1,0:T(8,128)(2,1)}, bf16[256,1024]{1,0:T(8,128)(2,1)}, u32[]{:S(2)}, u32[]{:S(2)}) collective-permute-start(bf16[256,1024]{1,0:T(8,128)(2,1)} %pad_maximum_fusion), channel_id=1, source_target_pairs={{0,4},{2,6},{4,8},{6,10},{8,12},{10,14},{12,16},{14,18},{16,20},{1... | collective-permute-start | bytes 1572872 | tf_op jit(solution)/shard_map/ppermute | solution.py:19
  106.3 0.0 slice-done
  106.3 0.9 reshape.258
  107.2 0.4 fusion.36
  107.6 0.0 copy-done.4
  107.6 0.0 copy-done.5
  107.6 0.9 subtract_convert_fusion
  108.6 5.3 %collective-permute-done.3 = bf16[256,1024]{1,0:T(8,128)(2,1)} collective-permute-done((bf16[256,1024]{1,0:T(8,128)(2,1)}, bf16[256,1024]{1,0:T(8,128)(2,1)}, u32[]{:S(2)}, u32[]{:S(2)}) %collective-permute-start.3) | collective-permute-done | bytes 524320 | tf_op jit(solution)/shard_map/ppermute | solution.py:19
  113.8 32.1 %collective-permute-done.2 = bf16[256,1024]{1,0:T(8,128)(2,1)} collective-permute-done((bf16[256,1024]{1,0:T(8,128)(2,1)}, bf16[256,1024]{1,0:T(8,128)(2,1)}, u32[]{:S(2)}, u32[]{:S(2)}) %collective-permute-start.2) | collective-permute-done | bytes 524320 | tf_op jit(solution)/shard_map/ppermute | solution.py:19
  146.0 1.4 maximum_maximum_fusion
  147.3 1.2 reshape.257
  148.5 0.0 copy-start.6
  148.5 2.0 %fusion.35 = (bf16[768,1,2,256]{3,2,1,0:T(2,128)(2,1)S(1)}, bf16[768,1,2,256]{3,2,1,0:T(2,128)(2,1)}) fusion(bf16[768,2,2,256]{3,2,1,0:T(2,128)(2,1)S(1)} %reshape.257), kind=kLoop, calls=%fused_computation.54 | loop fusion | bytes 3145728 | tf_op jit(solution)/shard_map/slice | solution.py:88
  150.5 0.6 copy.15
  151.1 2.4 %fusion.4 = (f32[2,2,256]{2,1,0:T(2,128)S(1)}, f32[2,768,256,2]{2,1,3,0:T(8,128)S(1)}) fusion(pred[256,768]{0,1:T(8,128)(4,1)} %fusion.26, bf16[256,2,2,128]{3,0,2,1:T(8,128)(2,1)} %get-tuple-element.8, bf16[256,2,2,128]{3,0,2,1:T(8,128)(2,1)S(1)} %copy-done.6, bf16[768,1,2,256]{3,2,1,0:T(2,128)(2,1)} %get-tuple-element.6), kind=kOutput, calls=%fused_computation.9 | convolution fusion | flops 406846464 | bytes 4657152 | tf_op jit(solution)/shard_map/qhgd,khd->hgqk/dot_general | solution.py:81
  153.5 1.2 divide_convert_fusion
  154.7 0.0 all-gather.5.cloned.1.call-done
  154.7 0.0 copy-start.1
  154.7 0.0 copy-start.8
  154.7 4.0 %multiply_reduce_fusion = (f32[256]{0:T(256)S(1)}, f32[256,2304]{1,0:T(8,128)S(1)}) fusion(bf16[256,1024]{0,1:T(8,128)(2,1)S(1)} %bitcast.49, bf16[1024,2304]{1,0:T(8,128)(2,1)} %all-gather.5.cloned.1.call-done), kind=kOutput, calls=%fused_computation.8 | convolution fusion | flops 1209138944 | bytes 7603200 | tf_op jit(solution)/shard_map/dot_general | solution.py:92
  158.7 0.0 copy-done.1
  158.7 0.0 copy-done.8
  158.7 1.4 fusion.15
  (20 shorter events, 0.2 us)
Async XLA Ops:
  6.5 11.3 %copy-start.9 = (s32[1,256]{1,0:T(1,128)S(1)}, s32[1,256]{1,0:T(1,128)}, u32[]{:S(2)}) copy-start(s32[1,256]{1,0:T(1,128)} %param.7) | copy-start | bytes 3076
  6.5 84.8 %copy-start = (bf16[1,256,2304]{2,1,0:T(8,128)(2,1)S(1)}, bf16[1,256,2304]{2,1,0:T(8,128)(2,1)}, u32[]{:S(2)}) copy-start(bf16[1,256,2304]{2,1,0:T(8,128)(2,1)} %param.6) | copy-start | bytes 3538948
  6.5 84.8 %copy-start.10 = (f32[2304]{0:T(1024)S(1)}, f32[2304]{0:T(1024)}, u32[]{:S(2)}) copy-start(f32[2304]{0:T(1024)} %param.8) | copy-start | bytes 27652
  6.5 84.8 %all-gather.3.cloned.1.call-start = ((), (), s32[]{:S(2)}) async-start(), calls=%async_computation | async-start | bytes 10027008 | tf_op jit(solution)/shard_map/all_gather | solution.py:57
  7.3 147.4 %all-gather.5.cloned.1.call-start = ((), (), s32[]{:S(2)}) async-start(), calls=%async_computation.1 | async-start | bytes 5013504 | tf_op jit(solution)/shard_map/all_gather | solution.py:94
  8.0 9.8 %collective-permute-start.1 = (s32[256]{0:T(256)}, s32[256]{0:T(256)S(1)}, u32[]{:S(2)}, u32[]{:S(2)}) collective-permute-start(s32[256]{0:T(256)} %bitcast.51), channel_id=1, source_target_pairs={{0,2},{2,4},{4,6},{6,8},{8,10},{10,12},{12,14},{14,16},{16,18},{18... | collective-permute-start | bytes 3080 | tf_op jit(solution)/shard_map/ppermute | solution.py:19
  11.7 6.1 %collective-permute-start = (s32[256]{0:T(256)}, s32[256]{0:T(256)S(1)}, u32[]{:S(2)}, u32[]{:S(2)}) collective-permute-start(s32[256]{0:T(256)} %bitcast.52), channel_id=1, source_target_pairs={{0,4},{2,6},{4,8},{6,10},{8,12},{10,14},{12,16},{14,18},{16,20},{1... | collective-permute-start | bytes 3080 | tf_op jit(solution)/shard_map/ppermute | solution.py:19
  96.6 1.5 copy-start.2
  96.6 1.5 copy-start.3
  98.0 8.3 %slice-start = ((f32[256,2048]{1,0:T(8,128)}), f32[256,1024]{1,0:T(8,128)S(1)}, s32[]{:S(2)}) async-start(f32[256,2048]{1,0:T(8,128)} %copy-done.2), calls=%async_computation.2 | async-start | bytes 2097152 | tf_op jit(solution)/shard_map/slice | solution.py:60
  100.7 6.9 %copy-start.4 = (f32[256,128]{1,0:T(8,128)S(1)}, f32[256,128]{1,0:T(8,128)}, u32[]{:S(2)}) copy-start(f32[256,128]{1,0:T(8,128)} %get-tuple-element.13) | copy-start | bytes 393220
  100.7 6.9 %copy-start.5 = (f32[256,128]{1,0:T(8,128)S(1)}, f32[256,128]{1,0:T(8,128)}, u32[]{:S(2)}) copy-start(f32[256,128]{1,0:T(8,128)} %get-tuple-element.14) | copy-start | bytes 393220
  100.7 13.2 %collective-permute-start.3 = (bf16[256,1024]{1,0:T(8,128)(2,1)}, bf16[256,1024]{1,0:T(8,128)(2,1)}, u32[]{:S(2)}, u32[]{:S(2)}) collective-permute-start(bf16[256,1024]{1,0:T(8,128)(2,1)} %pad_maximum_fusion), channel_id=1, source_target_pairs={{0,2},{2,4},{4,6},{6,8},{8,10},{10,12},{12,14},{14,16},{16,18},{18... | collective-permute-start | bytes 1572872 | tf_op jit(solution)/shard_map/ppermute | solution.py:19
  103.1 42.8 %collective-permute-start.2 = (bf16[256,1024]{1,0:T(8,128)(2,1)}, bf16[256,1024]{1,0:T(8,128)(2,1)}, u32[]{:S(2)}, u32[]{:S(2)}) collective-permute-start(bf16[256,1024]{1,0:T(8,128)(2,1)} %pad_maximum_fusion), channel_id=1, source_target_pairs={{0,4},{2,6},{4,8},{6,10},{8,12},{10,14},{12,16},{14,18},{16,20},{1... | collective-permute-start | bytes 1572872 | tf_op jit(solution)/shard_map/ppermute | solution.py:19
  148.5 2.5 %copy-start.6 = (bf16[256,2,2,128]{3,0,2,1:T(8,128)(2,1)S(1)}, bf16[256,2,2,128]{3,0,2,1:T(8,128)(2,1)}, u32[]{:S(2)}) copy-start(bf16[256,2,2,128]{3,0,2,1:T(8,128)(2,1)} %get-tuple-element.7) | copy-start | bytes 786436
  151.1 2.5 %copy-start.7 = (pred[256,768]{0,1:T(8,128)(4,1)S(1)}, pred[256,768]{0,1:T(8,128)(4,1)}, u32[]{:S(2)}) copy-start(pred[256,768]{0,1:T(8,128)(4,1)} %fusion.26) | copy-start | bytes 589828
  154.7 4.0 %copy-start.1 = (bf16[1,256,2304]{2,1,0:T(8,128)(2,1)S(1)}, bf16[1,256,2304]{2,1,0:T(8,128)(2,1)}, u32[]{:S(2)}) copy-start(bf16[1,256,2304]{2,1,0:T(8,128)(2,1)} %param.6) | copy-start | bytes 3538948
  154.7 4.0 %copy-start.8 = (f32[2304]{0:T(1024)S(1)}, f32[2304]{0:T(1024)}, u32[]{:S(2)}) copy-start(f32[2304]{0:T(1024)} %param.11) | copy-start | bytes 27652
Sparse Core Ops, SparseCore 0:
  9.6 81.6 all-gather.2
  93.6 58.4 all-gather.4
where the time goes:
time: 167 us
  waiting for transfers between devices  111 us (66%)
  between operations  13.7 us (8%)
  matrix products  12.8 us (8%)
  starting transfers between devices  12.5 us (7%)
  other arithmetic  10.6 us (6%)
  local copies, waits for them, and re-layouts  6.49 us (4%)
    all_gather x1, waiting for transfers between devices, per_device(): lax.all_gather(w_qkv, 'seq', axis=0, tiled=True)  72.1 us
    ppermute x4, waiting for transfers between devices, from_behind(): return lax.ppermute(block, axis, route)  37.4 us
    ppermute x4, starting transfers between devices, from_behind(): return lax.ppermute(block, axis, route)  12.5 us
    dot_general x1, matrix products, per_device(): jnp.dot(normed, lax.all_gather(w_qkv, 'seq', axis=0, tiled=True), preferr...  5.25 us
    dot_general x1, matrix products, per_device(): jnp.dot(attended, lax.all_gather(w_out, 'seq', axis=0, tiled=True), prefe...  3.96 us
  transfers between devices with their start and end apart: 6, of which 3 were waited for; matrix products, arithmetic and copies ran while one was open for 15% of the time, Pallas kernels for 0%

commit v1 on v0

--- a/solution.py
+++ b/solution.py
@@ -11,6 +11,11 @@
 DOCS = 16
 EPS = 1e-06
 CAP = 50.0
+
+
+def swapped_in(array, mesh_axis, along):
+    sent = jnp.stack([array] * lax.axis_size(mesh_axis))
+    return jnp.concatenate(lax.all_to_all(sent, mesh_axis, 0, 0), axis=along)
 
 
 def from_behind(block, axis, distance):
@@ -53,9 +58,7 @@
     id_blocks = [from_behind(own_ids, "seq", d) for d in range(hops, 0, -1)] + [own_ids]
     widened = hidden_in[0].astype(jnp.float32)
     normed = rms_scale(widened, pre_gain).astype(jnp.bfloat16)
-    projected = jnp.dot(
-        normed, lax.all_gather(w_qkv, "seq", axis=0, tiled=True), preferred_element_type=jnp.float32
-    )
+    projected = jnp.dot(normed, swapped_in(w_qkv, "seq", 0), preferred_element_type=jnp.float32)
     queries = rotary(
         projected[:, : Q_HEADS * HEAD].reshape(tok_rows, KV_HEADS, groups, HEAD), positions, 0
     ).astype(jnp.bfloat16)

time: 167 us -> 308 us (1.84)
  waiting for transfers between devices: 111 us -> 242 us
  local copies, waits for them, and re-layouts: 6.49 us -> 12.4 us
  starting transfers between devices: 12.5 us -> 17.2 us
    ppermute x4, waiting for transfers between devices: 37.4 us -> 241 us  [from_behind(): return lax.ppermute(block, axis, route)]
    all_gather x1 -> x0, waiting for transfers between devices: 72.1 us -> none  [per_device(): lax.all_gather(w_qkv, 'seq', axis=0, tiled=True)]
    all_to_all x0 -> x1, starting transfers between devices: none -> 6.6 us  [swapped_in(): return jnp.concatenate(lax.all_to_all(sent, mesh_axis, 0, 0), axis=along)]
    another operation x0 -> x1, local copies, waits for them, and re-layouts: none -> 5.93 us  [swapped_in(): sent = jnp.stack([array] * lax.axis_size(mesh_axis))]
  transfers between devices with their start and end apart: 6 -> 6, of which waited for: 3 -> 4; matrix products, arithmetic and copies ran while one was open for 15% -> 8% of each run, Pallas kernels for 0% -> 0%
where the time goes in v1:
time: 308 us; the launch traced here: 307 us
  waiting for transfers between devices  242 us (79%)
  starting transfers between devices  17.2 us (6%)
  between operations  13.7 us (4%)
  matrix products  12.8 us (4%)
  local copies, waits for them, and re-layouts  12.4 us (4%)
  other arithmetic  9.3 us (3%)
    ppermute x4, waiting for transfers between devices, from_behind(): return lax.ppermute(block, axis, route)  241 us
    ppermute x4, starting transfers between devices, from_behind(): return lax.ppermute(block, axis, route)  10.6 us
    all_to_all x1, starting transfers between devices, swapped_in(): return jnp.concatenate(lax.all_to_all(sent, mesh_axis, 0, 0), axis=along)  6.6 us
  transfers between devices with their start and end apart: 6, of which 4 were waited for; matrix products, arithmetic and copies ran while one was open for 8% of the time, Pallas kernels for 0%

profile of v1, /device:TPU:17, one launch (start us, length us, event | category | flops | bytes accessed | tf_op | source)
XLA Modules:
  0.0 307.2 jit_solution(5206192615280531052)
XLA Ops:
  6.5 5.9 %stack.2 = bf16[16,144,2048]{2,1,0:T(8,128)(2,1)} broadcast(bf16[144,2048]{1,0:T(8,128)(2,1)} %param.9), dimensions={1,2} | broadcast | bytes 10027008 | tf_op jit(solution)/shard_map/stack | solution.py:17
  12.5 6.6 %all-to-all-start = ((bf16[16,144,2048]{2,1,0:T(8,128)(2,1)}), bf16[16,144,2048]{2,1,0:T(8,128)(2,1)}, u32[]{:S(2)}, u32[]{:S(2)}) async-start(bf16[16,144,2048]{2,1,0:T(8,128)(2,1)} %stack.2), calls=%async_computation | async-start | bytes 18874368 | tf_op jit(solution)/shard_map/all_to_all | solution.py:18
  19.1 0.0 all-gather.2.cloned.1.call-start
  19.1 0.7 all-gather.2.cloned.1.call-update
  19.8 0.0 copy-done.9
  19.8 3.4 %collective-permute-start.1 = (s32[256]{0:T(256)S(1)}, s32[256]{0:T(256)S(1)}, u32[]{:S(2)}, u32[]{:S(2)}) collective-permute-start(s32[256]{0:T(256)S(1)} %bitcast.59), channel_id=1, source_target_pairs={{0,2},{2,4},{4,6},{6,8},{8,10},{10,12},{12,14},{14,16},{16,18},{18... | collective-permute-start | bytes 3080 | tf_op jit(solution)/shard_map/ppermute | solution.py:24
  23.2 3.1 %collective-permute-start = (s32[256]{0:T(256)S(1)}, s32[256]{0:T(256)S(1)}, u32[]{:S(2)}, u32[]{:S(2)}) collective-permute-start(s32[256]{0:T(256)S(1)} %bitcast.60), channel_id=1, source_target_pairs={{0,4},{2,6},{4,8},{6,10},{8,12},{10,14},{12,16},{14,18},{16,20},{1... | collective-permute-start | bytes 3080 | tf_op jit(solution)/shard_map/ppermute | solution.py:24
  26.3 0.0 copy-done
  26.4 0.3 fusion.2
  26.7 1.2 multiply_cosine_fusion
  27.9 31.1 %collective-permute-done.1 = s32[256]{0:T(256)S(1)} collective-permute-done((s32[256]{0:T(256)S(1)}, s32[256]{0:T(256)S(1)}, u32[]{:S(2)}, u32[]{:S(2)}) %collective-permute-start.1) | collective-permute-done | bytes 1056 | tf_op jit(solution)/shard_map/ppermute | solution.py:24
  59.1 192.9 %collective-permute-done = s32[256]{0:T(256)S(1)} collective-permute-done((s32[256]{0:T(256)S(1)}, s32[256]{0:T(256)S(1)}, u32[]{:S(2)}, u32[]{:S(2)}) %collective-permute-start) | collective-permute-done | bytes 1056 | tf_op jit(solution)/shard_map/ppermute | solution.py:24
  252.0 1.4 fusion.28
  253.4 0.0 all-to-all-done
  253.4 0.0 copy-done.10
  253.4 5.2 %fusion.18 = f32[256,2048]{1,0:T(8,128)S(1)} fusion(bf16[2304,2048]{1,0:T(8,128)(2,1)} %bitcast.3, bf16[1,256,2304]{2,1,0:T(8,128)(2,1)S(1)} %copy-done, f32[2304]{0:T(1024)S(1)} %copy-done.10, f32[256]{0:T(256)S(1)} %add_rsqrt_fusion.1), kind=kOutput, calls=%fused_computation.20 | convolution fusion | flops 2418278400 | bytes 12724224 | tf_op jit(solution)/shard_map/dot_general | solution.py:61
  258.7 0.0 copy-start.2
  258.7 0.0 copy-start.3
  258.8 1.4 reshape.276
  260.1 0.0 copy-done.2
  260.1 0.0 copy-done.3
  260.2 1.4 subtract_convert_fusion.1
  261.6 0.3 pad_maximum_fusion.1
  261.9 0.9 pad_maximum_fusion
  262.8 2.0 collective-permute-start.3
  264.8 2.1 collective-permute-start.2
  266.9 0.0 slice-done
  266.9 0.9 reshape.278
  267.8 0.4 fusion.38
  268.2 0.0 copy-done.4
  268.2 0.0 copy-done.5
  268.2 0.9 subtract_convert_fusion
  269.2 4.6 %collective-permute-done.3 = bf16[256,1024]{1,0:T(8,128)(2,1)} collective-permute-done((bf16[256,1024]{1,0:T(8,128)(2,1)}, bf16[256,1024]{1,0:T(8,128)(2,1)}, u32[]{:S(2)}, u32[]{:S(2)}) %collective-permute-start.3) | collective-permute-done | bytes 524320 | tf_op jit(solution)/shard_map/ppermute | solution.py:24
  273.8 12.3 %collective-permute-done.2 = bf16[256,1024]{1,0:T(8,128)(2,1)} collective-permute-done((bf16[256,1024]{1,0:T(8,128)(2,1)}, bf16[256,1024]{1,0:T(8,128)(2,1)}, u32[]{:S(2)}, u32[]{:S(2)}) %collective-permute-start.2) | collective-permute-done | bytes 524320 | tf_op jit(solution)/shard_map/ppermute | solution.py:24
  286.1 1.4 maximum_maximum_fusion
  287.5 1.2 reshape.277
  288.6 0.0 copy-start.6
  288.7 2.0 fusion.37
  290.6 0.6 copy.15
  291.2 0.0 copy-done.6
  291.2 0.0 copy-start.7
  291.2 2.4 fusion.6
  293.7 1.2 divide_convert_fusion
  294.8 0.0 all-gather.2.cloned.1.call-done
  294.9 0.0 copy-start.1
  294.9 0.0 copy-start.8
  294.9 4.0 %multiply_reduce_fusion = (f32[256]{0:T(256)S(1)}, f32[256,2304]{1,0:T(8,128)S(1)}) fusion(bf16[256,1024]{0,1:T(8,128)(2,1)S(1)} %bitcast.57, bf16[1024,2304]{1,0:T(8,128)(2,1)} %all-gather.2.cloned.1.call-done), kind=kOutput, calls=%fused_computation.9 | convolution fusion | flops 1209138944 | bytes 7603200 | tf_op jit(solution)/shard_map/dot_general | solution.py:95
  298.9 1.4 fusion.20
  (20 shorter events, 0.2 us)
Async XLA Ops:
  12.5 7.3 %copy-start.9 = (s32[1,256]{1,0:T(1,128)S(1)}, s32[1,256]{1,0:T(1,128)}, u32[]{:S(2)}) copy-start(s32[1,256]{1,0:T(1,128)} %param.7) | copy-start | bytes 3076
  12.5 13.9 %copy-start = (bf16[1,256,2304]{2,1,0:T(8,128)(2,1)S(1)}, bf16[1,256,2304]{2,1,0:T(8,128)(2,1)}, u32[]{:S(2)}) copy-start(bf16[1,256,2304]{2,1,0:T(8,128)(2,1)} %param.6) | copy-start | bytes 3538948
  12.5 240.9 %copy-start.10 = (f32[2304]{0:T(1024)S(1)}, f32[2304]{0:T(1024)}, u32[]{:S(2)}) copy-start(f32[2304]{0:T(1024)} %param.8) | copy-start | bytes 27652
  12.5 240.9 %all-to-all-start = ((bf16[16,144,2048]{2,1,0:T(8,128)(2,1)}), bf16[16,144,2048]{2,1,0:T(8,128)(2,1)}, u32[]{:S(2)}, u32[]{:S(2)}) async-start(bf16[16,144,2048]{2,1,0:T(8,128)(2,1)} %stack.2), calls=%async_computation | async-start | bytes 18874368 | tf_op jit(solution)/shard_map/all_to_all | solution.py:18
  19.1 275.8 %all-gather.2.cloned.1.call-start = ((), (), s32[]{:S(2)}) async-start(), calls=%async_computation.1 | async-start | bytes 5013504 | tf_op jit(solution)/shard_map/all_gather | solution.py:97
  19.8 39.3 %collective-permute-start.1 = (s32[256]{0:T(256)S(1)}, s32[256]{0:T(256)S(1)}, u32[]{:S(2)}, u32[]{:S(2)}) collective-permute-start(s32[256]{0:T(256)S(1)} %bitcast.59), channel_id=1, source_target_pairs={{0,2},{2,4},{4,6},{6,8},{8,10},{10,12},{12,14},{14,16},{16,18},{18... | collective-permute-start | bytes 3080 | tf_op jit(solution)/shard_map/ppermute | solution.py:24
  23.2 228.8 %collective-permute-start = (s32[256]{0:T(256)S(1)}, s32[256]{0:T(256)S(1)}, u32[]{:S(2)}, u32[]{:S(2)}) collective-permute-start(s32[256]{0:T(256)S(1)} %bitcast.60), channel_id=1, source_target_pairs={{0,4},{2,6},{4,8},{6,10},{8,12},{10,14},{12,16},{14,18},{16,20},{1... | collective-permute-start | bytes 3080 | tf_op jit(solution)/shard_map/ppermute | solution.py:24
  258.7 1.5 copy-start.2
  258.7 1.5 copy-start.3
  260.1 6.8 %slice-start = ((f32[256,2048]{1,0:T(8,128)}), f32[256,1024]{1,0:T(8,128)S(1)}, s32[]{:S(2)}) async-start(f32[256,2048]{1,0:T(8,128)} %copy-done.2), calls=%async_computation.2 | async-start | bytes 2097152 | tf_op jit(solution)/shard_map/slice | solution.py:63
  262.8 5.4 %copy-start.4 = (f32[256,128]{1,0:T(8,128)S(1)}, f32[256,128]{1,0:T(8,128)}, u32[]{:S(2)}) copy-start(f32[256,128]{1,0:T(8,128)} %get-tuple-element.13) | copy-start | bytes 393220
  262.8 5.5 %copy-start.5 = (f32[256,128]{1,0:T(8,128)S(1)}, f32[256,128]{1,0:T(8,128)}, u32[]{:S(2)}) copy-start(f32[256,128]{1,0:T(8,128)} %get-tuple-element.14) | copy-start | bytes 393220
  262.8 11.0 %collective-permute-start.3 = (bf16[256,1024]{1,0:T(8,128)(2,1)}, bf16[256,1024]{1,0:T(8,128)(2,1)}, u32[]{:S(2)}, u32[]{:S(2)}) collective-permute-start(bf16[256,1024]{1,0:T(8,128)(2,1)} %pad_maximum_fusion), channel_id=1, source_target_pairs={{0,2},{2,4},{4,6},{6,8},{8,10},{10,12},{12,14},{14,16},{16,18},{18... | collective-permute-start | bytes 1572872 | tf_op jit(solution)/shard_map/ppermute | solution.py:24
  264.8 21.3 %collective-permute-start.2 = (bf16[256,1024]{1,0:T(8,128)(2,1)}, bf16[256,1024]{1,0:T(8,128)(2,1)}, u32[]{:S(2)}, u32[]{:S(2)}) collective-permute-start(bf16[256,1024]{1,0:T(8,128)(2,1)} %pad_maximum_fusion), channel_id=1, source_target_pairs={{0,4},{2,6},{4,8},{6,10},{8,12},{10,14},{12,16},{14,18},{16,20},{1... | collective-permute-start | bytes 1572872 | tf_op jit(solution)/shard_map/ppermute | solution.py:24
  288.6 2.5 copy-start.6
  291.2 2.5 copy-start.7
  294.9 4.0 %copy-start.1 = (bf16[1,256,2304]{2,1,0:T(8,128)(2,1)S(1)}, bf16[1,256,2304]{2,1,0:T(8,128)(2,1)}, u32[]{:S(2)}) copy-start(bf16[1,256,2304]{2,1,0:T(8,128)(2,1)} %param.6) | copy-start | bytes 3538948
  294.9 4.0 %copy-start.8 = (f32[2304]{0:T(1024)S(1)}, f32[2304]{0:T(1024)}, u32[]{:S(2)}) copy-start(f32[2304]{0:T(1024)} %param.11) | copy-start | bytes 27652
Sparse Core Ops, SparseCore 0:
  22.2 164.0 all-gather.1
